TPU v7x, 32 devices: a whole 2x2x4 slice. The times are simulated.
32 devices in a mesh: pair: 4 (over x, core), aux: 8 (over z, y).
Axes of the slice: x: 2, y: 2, z: 4, core: 2. Of those that a mesh axis runs over, the one named last changes fastest.
Arguments:
- left_active: bfloat16 [40, 128, 61440], P('pair', None, 'aux'), may hold values from -0.375 to 0.375
- right_active: bfloat16 [40, 128, 61440], P('pair', None, 'aux'), may hold values from -0.375 to 0.375
- amps_active: bfloat16 [40, 128, 128], P('pair', 'aux'), may hold values from -0.5 to 0.5
- rank_active: int32 [40], P('pair'), may hold values from 80 to 128, as said below
- gap_active: float32 [40], P('pair'), may hold values from 0.5 to 2
- energy_active: float32 [40, 128], P('pair'), may hold values from 0.5 to 4
- intersect_active: bfloat16 [40, 4, 128, 128], P('pair'), may hold values from -0.75 to 0.75
- fock_active: float32 [40, 4], P('pair'), may hold values from -2 to 2
- neighbor_active: int32 [40, 4], P('pair'), may hold values from 0 to 39
- left_env: bfloat16 [16, 48, 61440], P('pair', None, 'aux'), may hold values from -0.375 to 0.375
- right_env: bfloat16 [16, 48, 61440], P('pair', None, 'aux'), may hold values from -0.375 to 0.375
- amps_env: bfloat16 [16, 48, 48], P('pair', 'aux'), may hold values from -0.875 to 0.875
- rank_env: int32 [16], P('pair'), may hold values from 24 to 48, as said below
- gap_env: float32 [16], P('pair'), may hold values from 0.5 to 2
- energy_env: float32 [16, 48], P('pair'), may hold values from 0.5 to 4
- intersect_env: bfloat16 [16, 4, 48, 48], P('pair'), may hold values from -1.25 to 1.25
- fock_env: float32 [16, 4], P('pair'), may hold values from -2 to 2
- neighbor_env: int32 [16, 4], P('pair'), may hold values from 0 to 15
Outputs:
- new_active: float32 [40, 128, 128], P('pair', 'aux')
- new_env: float32 [16, 48, 48], P('pair', 'aux')
Inputs may be any that keep to these rules, and one draw needn't show every extreme that they name: `rank_active`: multiples of 8; the first active pair has rank 128. `rank_env`: multiples of 8; the first environment pair has rank 48.
All inputs are finite; a program needn't handle non-finite values.
Results may differ from a plain program's by a relative error of at most 0.0041.
Values may be sent and summed in bfloat16 or wider, within the bound.
A program may use at most 128 MiB of HBM per device.

v0:
```python
import functools

import jax
import jax.numpy as jnp
from jax import lax
from jax.experimental import pallas as pl
from jax.experimental.pallas import tpu as pltpu
from jax.sharding import PartitionSpec as P

BF = jnp.bfloat16
F32 = jnp.float32
LANES = 128
AHEAD = 4
WARM = 5
LATE = 2


def dot_nt(x, y):
    return lax.dot_general(x, y, (((1,), (1,)), ((), ())), preferred_element_type=F32)


def split(x):
    hi = x.astype(BF)
    return hi, (x - hi.astype(F32)).astype(BF)


def iota2(shape, dim):
    return lax.broadcasted_iota(jnp.int32, shape, dim)


def half_couple(over, near, fock, place, rows, step):
    width = over[0].shape[1]
    pick = (iota2((step, width), 1) == place * rows + iota2((step, width), 0)) & (
        iota2((step, width), 0) < rows
    )
    pick = jnp.where(pick, F32(1.0), F32(0.0))
    lefts, rights = [], []
    for k in range(len(over)):
        both = dot_nt(jnp.concatenate([pick, near[k]], axis=0).astype(BF), over[k])
        lefts.append(both[:step])
        rights.append(both[step:] * fock[k])
    return jnp.concatenate(lefts, axis=0).astype(BF), jnp.concatenate(rights, axis=0).astype(BF)


def dot_tn(x, y):
    return lax.dot_general(x, y, (((0,), (0,)), ((), ())), preferred_element_type=F32)


def far_first(n):
    return sorted(range(1, n), key=lambda d: -min(d, n - d))


def kernel(
    n_pair, n_aux,
    la, ra, aa, rka_h, gpa_h, ena_h, ina, fka_h, nba_h,
    le, re, ae_h, rke_h, gpe_h, ene_h, ine_h, fke_h, nbe_h,
    oa, oe,
    lbuf, rbuf, lebuf, rebuf, inbuf, aabuf, ae, ena, ene, ine,
    rka, gpa, fka, nba, rke, gpe, fke, nbe,
    mine, own, around, mine_e, around_e,
    terms, out_a, in_a, terms_e, out_e, in_e, den, den_e,
    lefts, rights,
    lr_sem, lre_sem, in_sem, small_sem,
    own_send, own_recv, pair_send, pair_recv, paire_send, paire_recv,
    a_send, a_recv, e_send, e_recv,
):
    pairs, rows, full = mine.shape
    rows_e, pairs_e, full_e = ae.shape
    pad_e = mine_e.shape[1]
    count = nba.shape[0]
    warm = min(WARM, pairs - 1)
    late = pairs - LATE
    me = lax.axis_index("aux")
    my_pair = lax.axis_index("pair")
    order = far_first(n_aux)

    def load_lr(p):
        return (
            pltpu.make_async_copy(la.at[p], lbuf.at[p], lr_sem.at[p, 0]),
            pltpu.make_async_copy(ra.at[p], rbuf.at[p], lr_sem.at[p, 1]),
        )

    def load_e(q):
        return (
            pltpu.make_async_copy(le.at[q], lebuf.at[q], lre_sem.at[q, 0]),
            pltpu.make_async_copy(re.at[q], rebuf.at[q], lre_sem.at[q, 1]),
        )

    def start_load(i):
        if isinstance(i, int):
            if i < pairs:
                for copy in load_lr(i):
                    copy.start()
            elif i < pairs + pairs_e:
                for copy in load_e(i - pairs):
                    copy.start()
        else:
            @pl.when(i < pairs)
            def _():
                for copy in load_lr(i):
                    copy.start()

            @pl.when((i >= pairs) & (i < pairs + pairs_e))
            def _():
                for copy in load_e(i - pairs):
                    copy.start()

    small = [(aa, aabuf), (rka_h, rka), (ae_h, ae), (rke_h, rke)]
    rest = [
        (gpa_h, gpa), (ena_h, ena), (fka_h, fka), (nba_h, nba), (gpe_h, gpe), (ene_h, ene),
        (ine_h, ine), (fke_h, fke), (nbe_h, nbe),
    ]
    copies = [pltpu.make_async_copy(x, y, small_sem.at[i]) for i, (x, y) in enumerate(small + rest)]
    for copy in copies[: len(small)]:
        copy.start()
    barrier = pltpu.get_barrier_semaphore()
    for d in order:
        pl.semaphore_signal(barrier, inc=1, device_id={"aux": lax.rem(me + d, n_aux)}, device_id_type=pl.DeviceIdType.MESH)
    for d in range(1, n_pair):
        pl.semaphore_signal(barrier, inc=1, device_id={"pair": lax.rem(my_pair + d, n_pair)}, device_id_type=pl.DeviceIdType.MESH)
    for i in range(AHEAD):
        start_load(i)
    for copy in copies[len(small) :]:
        copy.start()
    load_in = pltpu.make_async_copy(ina, inbuf, in_sem)
    load_in.start()
    for copy in copies[: len(small)]:
        copy.wait()

    def inside(rank, start, shape):
        return (start + iota2(shape, 0) < rank) & (iota2(shape, 1) < rank)

    for p in range(pairs):
        keep = inside(rka[p], me * rows, (rows, full))
        block = jnp.where(keep, aabuf[p].astype(F32), F32(0.0)).astype(BF)
        mine[p] = block
        own[me, p] = block
        around[my_pair * pairs + p] = block
    mine_e[...] = jnp.zeros(mine_e.shape, F32)
    amps_e = ae[...].astype(F32)
    for p in range(pairs_e):
        keep = inside(rke[p], me * rows_e, (rows_e, full_e))
        mine_e[p, :rows_e, :full_e] = jnp.where(keep, amps_e[:, p, :], F32(0.0))
    for p in range(pairs_e):
        around_e[my_pair * pairs_e + p] = mine_e[p]
    out_e[...] = jnp.zeros(out_e.shape, out_e.dtype)

    def to_own(d, slot):
        return pltpu.make_async_remote_copy(
            src_ref=mine, dst_ref=own.at[slot],
            send_sem=own_send.at[d - 1], recv_sem=own_recv.at[d - 1],
            device_id={"aux": lax.rem(me + d, n_aux)}, device_id_type=pl.DeviceIdType.MESH,
        )

    def to_pair(d, slot):
        return pltpu.make_async_remote_copy(
            src_ref=mine, dst_ref=around.at[pl.ds(slot * pairs, pairs)],
            send_sem=pair_send.at[d - 1], recv_sem=pair_recv.at[d - 1],
            device_id={"pair": lax.rem(my_pair + d, n_pair)}, device_id_type=pl.DeviceIdType.MESH,
        )

    def to_pair_e(d, slot):
        return pltpu.make_async_remote_copy(
            src_ref=mine_e, dst_ref=around_e.at[pl.ds(slot * pairs_e, pairs_e)],
            send_sem=paire_send.at[d - 1], recv_sem=paire_recv.at[d - 1],
            device_id={"pair": lax.rem(my_pair + d, n_pair)}, device_id_type=pl.DeviceIdType.MESH,
        )

    pl.semaphore_wait(barrier, n_aux - 1 + n_pair - 1)
    for d in order:
        to_own(d, me).start()
    for d in range(1, n_pair):
        to_pair(d, my_pair).start()
        to_pair_e(d, my_pair).start()

    def denominators(energy, gap, start, height, wide):
        line = energy + jnp.zeros((height, wide), F32)
        diag = iota2((height, wide), 1) == start + iota2((height, wide), 0)
        mine_rows = jnp.sum(jnp.where(diag, line, F32(0.0)), axis=1, keepdims=True)
        return line + mine_rows + gap

    def a_copy(d, p, group):
        peer = lax.rem(me + d, n_aux)
        return pltpu.make_async_remote_copy(
            src_ref=out_a.at[peer, p], dst_ref=in_a.at[d - 1, p],
            send_sem=a_send.at[d - 1, group], recv_sem=a_recv.at[d - 1, group],
            device_id={"aux": peer}, device_id_type=pl.DeviceIdType.MESH,
        )

    def e_copy(d):
        peer = lax.rem(me + d, n_aux)
        return pltpu.make_async_remote_copy(
            src_ref=out_e.at[peer], dst_ref=in_e.at[d - 1],
            send_sem=e_send.at[d - 1], recv_sem=e_recv.at[d - 1],
            device_id={"aux": peer}, device_id_type=pl.DeviceIdType.MESH,
        )

    def send_pair(p, group):
        for d in order:
            a_copy(d, p, group).start()

    def integrals(p):
        for copy in load_lr(p):
            copy.wait()
        return dot_nt(lbuf[p], rbuf[p])

    def ladder(p):
        terms[p] = integrals(p).reshape(n_aux, rows, full)

    def prepare(p):
        left, right = half_couple(
            [inbuf[p, k] for k in range(count)],
            [around[nba[k, p]].astype(F32) for k in range(count)],
            [fka[k, p] for k in range(count)],
            me, rows, rows,
        )
        lefts[p] = left
        rights[p] = right

    def finish(p):
        base = terms[p].reshape(full, full)
        amps = own[:, p].astype(F32).reshape(full, full).astype(BF)
        half = base + dot_nt(base.astype(BF), amps)
        total = base + dot_tn(
            jnp.concatenate([amps, lefts[p]], axis=0),
            jnp.concatenate([half.astype(BF), rights[p]], axis=0),
        )
        terms[p] = total.reshape(n_aux, rows, full)
        for j in range(n_aux):
            out_a[j, p] = total[j * rows : (j + 1) * rows].astype(BF)

    def warm_step(p, carry):
        start_load(p + AHEAD)
        ladder(p)
        return carry

    lax.fori_loop(0, warm, warm_step, 0)

    for copy in copies[len(small) :]:
        copy.wait()
    load_in.wait()
    for d in range(1, n_pair):
        slot = lax.rem(my_pair + n_pair - d, n_pair)
        to_pair(d, slot).wait_recv()
        to_pair_e(d, slot).wait_recv()

    def prepare_step(p, carry):
        prepare(p)
        return carry

    lax.fori_loop(0, pairs, prepare_step, 0)
    for q in range(pairs_e):
        left, right = half_couple(
            [ine[q, k] for k in range(count)],
            [around_e[nbe[q, k]][:, :full_e] for k in range(count)],
            [fke[q, k] for k in range(count)],
            me, rows_e, pad_e,
        )
        terms_e[q] = dot_tn(left, right)
    for p in range(pairs):
        den[p] = denominators(ena[pl.ds(p, 1), :], gpa[p], me * rows, rows, full)
    for p in range(pairs_e):
        den_e[p] = denominators(ene[pl.ds(p, 1), :], gpe[p], me * rows_e, rows_e, full_e)
    for d in range(1, n_aux):
        to_own(d, lax.rem(me + n_aux - d, n_aux)).wait_recv()

    twos = min(pairs - 1 - warm, max(0, warm - 1))

    def catch_step(i, carry):
        p = warm + i
        start_load(p + AHEAD)

        @pl.when(i > 0)
        def _():
            send_pair(2 * i - 2, 0)
            send_pair(2 * i - 1, 0)

        ladder(p)
        finish(2 * i)
        finish(2 * i + 1)
        return carry

    lax.fori_loop(0, twos, catch_step, 0)
    done = 2 * twos
    sent = max(0, done - 2)
    for p in range(warm + twos, pairs):
        start_load(p + AHEAD)
        for q in range(sent, done):
            send_pair(q, int(q >= late))
        sent = done
        ladder(p)
        if done < p:
            finish(done)
            done += 1
    for i in range(pairs + AHEAD, pairs + pairs_e):
        start_load(i)
    for q in range(sent, done):
        send_pair(q, int(q >= late))
    sent = done
    while done < pairs:
        finish(done)
        done += 1
    for q in range(pairs_e):
        for copy in load_e(q):
            copy.wait()
        total = terms_e[q] + dot_nt(lebuf[q], rebuf[q])
        terms_e[q] = total
        for j in range(n_aux):
            out_e[j, q, :rows_e, :full_e] = total[j * rows_e : (j + 1) * rows_e, :].astype(out_e.dtype)
        if q == 0:
            for p in range(sent, pairs):
                send_pair(p, int(p >= late))

    def combine(p):
        total = terms[p, me]
        for d in range(1, n_aux):
            total = total + in_a[d - 1, p].astype(F32)
        keep = inside(rka[p], me * rows, (rows, full))
        oa[p] = jnp.where(keep, mine[p].astype(F32) - total / den[p], F32(0.0))

    def arrived(group):
        block = in_a.at[:, pl.ds(0, late)] if group == 0 else in_a.at[:, pl.ds(late, pairs - late)]
        return [
            pltpu.make_async_copy(block.at[d - 1], block.at[d - 1], a_recv.at[d - 1, group])
            for d in range(1, n_aux)
        ]

    for d in order:
        e_copy(d).start()
    for copy in arrived(0):
        copy.wait()
    for p in range(late):
        combine(p)
    for copy in arrived(1):
        copy.wait()
    for p in range(late, pairs):
        combine(p)

    for d in range(1, n_aux):
        e_copy(d).wait_recv()
    for p in range(pairs_e):
        total = out_e[me, p].astype(F32)
        for d in range(1, n_aux):
            total = total + in_e[d - 1, p].astype(F32)
        keep = inside(rke[p], me * rows_e, (rows_e, full_e))
        oe[:, p, :] = jnp.where(
            keep, mine_e[p, :rows_e, :full_e] - total[:rows_e, :full_e] / den_e[p], F32(0.0)
        )

    for d in range(1, n_pair):
        to_pair(d, my_pair).wait_send()
        to_pair_e(d, my_pair).wait_send()
    for d in range(1, n_aux):
        to_own(d, me).wait_send()
        e_copy(d).wait_send()
        for group, block in ((0, in_a.at[:, pl.ds(0, late)]), (1, in_a.at[:, pl.ds(late, pairs - late)])):
            pltpu.make_async_copy(block.at[d - 1], block.at[d - 1], a_send.at[d - 1, group]).wait()


def shards(n_pair, n_aux, *args):
    la, ra, aa = args[:3]
    ina = args[6]
    le, re, ae = args[9:12]
    pairs, rows, full = aa.shape
    pairs_e, rows_e, full_e = ae.shape
    pad_e = -(-rows_e // 8) * 8
    hbm = pl.BlockSpec(memory_space=pl.ANY)
    vmem = pl.BlockSpec(memory_space=pltpu.VMEM)
    dma = pltpu.SemaphoreType.DMA
    args = list(args)
    for i in (7, 8):
        args[i] = args[i].T
    args[11] = ae.transpose(1, 0, 2)

    def like(space, *which):
        return [space(args[i].shape, args[i].dtype) for i in which]

    new_a, new_e = pl.pallas_call(
        functools.partial(kernel, n_pair, n_aux),
        out_shape=(
            pltpu.VMEM(aa.shape, F32),
            pltpu.VMEM(args[11].shape, F32),
        ),
        in_specs=[hbm] * len(args),
        out_specs=(vmem, vmem),
        scratch_shapes=like(pltpu.VMEM, 0, 1, 9, 10, 6, 2, 11, 5, 14, 15)
        + like(pltpu.SMEM, 3, 4, 7, 8, 12, 13, 16, 17)
        + [
            pltpu.VMEM((pairs, rows, full), BF),
            pltpu.VMEM((n_aux, pairs, rows, full), BF),
            pltpu.VMEM((n_pair * pairs, rows, full), BF),
            pltpu.VMEM((pairs_e, pad_e, LANES), F32),
            pltpu.VMEM((n_pair * pairs_e, pad_e, LANES), F32),
            pltpu.VMEM((pairs, n_aux, rows, full), F32),
            pltpu.VMEM((n_aux, pairs, rows, full), BF),
            pltpu.VMEM((n_aux - 1, pairs, rows, full), BF),
            pltpu.VMEM((pairs_e, full_e, full_e), F32),
            pltpu.VMEM((n_aux, pairs_e, pad_e, LANES), F32),
            pltpu.VMEM((n_aux - 1, pairs_e, pad_e, LANES), F32),
            pltpu.VMEM((pairs, rows, full), F32),
            pltpu.VMEM((pairs_e, rows_e, full_e), F32),
            pltpu.VMEM((pairs, ina.shape[1] * rows, full), BF),
            pltpu.VMEM((pairs, ina.shape[1] * rows, full), BF),
            dma((pairs, 2)),
            dma((pairs_e, 2)),
            dma,
            dma((13,)),
            dma((n_aux - 1,)),
            dma((n_aux - 1,)),
            dma((n_pair - 1,)),
            dma((n_pair - 1,)),
            dma((n_pair - 1,)),
            dma((n_pair - 1,)),
            dma((n_aux - 1, 2)),
            dma((n_aux - 1, 2)),
            dma((n_aux - 1,)),
            dma((n_aux - 1,)),
        ],
        compiler_params=pltpu.CompilerParams(
            collective_id=0, has_side_effects=True, vmem_limit_bytes=60 * 1024 * 1024
        ),
        name="update",
    )(*args)
    return new_a, new_e.transpose(1, 0, 2)


def solution(mesh):
    n_pair, n_aux = mesh.shape["pair"], mesh.shape["aux"]
    level = (
        P("pair", None, "aux"),
        P("pair", None, "aux"),
        P("pair", "aux", None),
        P("pair"),
        P("pair"),
        P("pair", None),
        P("pair", None, None, None),
        P("pair", None),
        P("pair", None),
    )
    return jax.shard_map(
        functools.partial(shards, n_pair, n_aux),
        mesh=mesh,
        in_specs=level + level,
        out_specs=(P("pair", "aux", None), P("pair", "aux", None)),
        check_vma=False,
    )
```

profile of v0, /device:TPU:0, one launch (start us, length us, event | category | flops | bytes accessed | tf_op | source)
XLA Modules:
  0.0 31.4 jit_solution(14988640586872907383)
XLA Ops:
  0.6 29.5 %update.1 = (f32[10,16,128]{2,1,0:T(8,128)S(1)}, f32[6,4,48]{2,1,0:T(4,128)S(1)}) custom-call(bf16[10,128,7680]{2,1,0:T(8,128)(2,1)} %la.1, bf16[10,128,7680]{2,1,0:T(8,128)(2,1)} %ra.1, bf16[10,16,128]{2,1,0:T(8,128)(2,1)} %aa.1, s32[10]{0:T(128)} %rka_h.1, f32[10]{0:T(128)} %gpa_h.1, f32[10,128]{1,0:T(8,128)} %ena_h.1, bf16[10,4,128,128]{3,2,1,0:T(8,128)(2,1)} %ina.1, ...), custom_call_target="tpu_custom_call" | custom-call | tf_op jit(solution)/shard_map/update/pallas_call | solution.py:378
  30.1 0.6 %copy.22 = f32[10,16,128]{2,1,0:T(8,128)} copy(f32[10,16,128]{2,1,0:T(8,128)S(1)} %get-tuple-element.6) | data formatting | bytes 163840
  30.8 0.6 %copy.23 = f32[4,6,48]{2,0,1:T(4,128)} copy(f32[4,6,48]{2,0,1:T(4,128)S(1)} %bitcast.4) | data formatting | bytes 9216
where the time goes:
time: 31.5 us; the launch traced here: 31.4 us
  Pallas kernels  29.5 us (94%)
  local copies, waits for them, and re-layouts  1.24 us (4%)
  between operations  0.65 us (2%)
    pallas_call x1, Pallas kernels, shards(): pl.pallas_call(functools.partial(kernel, n_pair, n_aux), out_shape=(pltpu...  29.5 us
    unnamed x2, local copies, waits for them, and re-layouts  1.24 us

commit v1 on v0

v1 whole, which is shorter than its diff:
```python
import functools

import jax
import jax.numpy as jnp
from jax import lax
from jax.experimental import pallas as pl
from jax.experimental.pallas import tpu as pltpu
from jax.sharding import PartitionSpec as P

BF = jnp.bfloat16
F32 = jnp.float32
LANES = 128
AHEAD = 3
FIRST = 1
WARM = 5
LATE = 2
EDT = jnp.bfloat16


def dot_nt(x, y):
    return lax.dot_general(x, y, (((1,), (1,)), ((), ())), preferred_element_type=F32)


def split(x):
    hi = x.astype(BF)
    return hi, (x - hi.astype(F32)).astype(BF)


def iota2(shape, dim):
    return lax.broadcasted_iota(jnp.int32, shape, dim)


def half_couple(over, near, fock, place, rows, step):
    width = over[0].shape[1]
    pick = (iota2((step, width), 1) == place * rows + iota2((step, width), 0)) & (
        iota2((step, width), 0) < rows
    )
    pick = jnp.where(pick, F32(1.0), F32(0.0))
    lefts, rights = [], []
    for k in range(len(over)):
        both = dot_nt(jnp.concatenate([pick, near[k]], axis=0).astype(BF), over[k])
        lefts.append(both[:step])
        rights.append(both[step:] * fock[k])
    return jnp.concatenate(lefts, axis=0).astype(BF), jnp.concatenate(rights, axis=0).astype(BF)


def dot_tn(x, y):
    return lax.dot_general(x, y, (((0,), (0,)), ((), ())), preferred_element_type=F32)


def far_first(n):
    return sorted(range(1, n), key=lambda d: -min(d, n - d))


def kernel(
    n_pair, n_aux,
    la, ra, aa, rka_h, gpa_h, ena_h, ina, fka_h, nba_h,
    le, re, ae_h, rke_h, gpe_h, ene_h, ine_h, fke_h, nbe_h,
    oa, oe,
    buf, ebuf, inbuf, aabuf, ae, ena, ene, ine,
    rka, gpa, fka, nba, rke, gpe, fke, nbe,
    mine, own, around, mine_e, around_e,
    terms, out_a, in_a, terms_e, out_e, in_e, den, den_e, lefts, rights,
    load_sem, env_sem, pool, send_sem, recv_sem,
):
    pairs, rows, full = mine.shape
    rows_e, pairs_e, full_e = ae.shape
    pad_e = mine_e.shape[1]
    count = nba.shape[0]
    warm = min(WARM, pairs - 1)
    first = min(FIRST, warm)
    late = pairs - LATE
    ring = load_sem.shape[0]
    me = lax.axis_index("aux")
    my_pair = lax.axis_index("pair")
    order = far_first(n_aux)
    mesh_id = pl.DeviceIdType.MESH

    def landed(block, sem):
        pltpu.make_async_copy(block, block, sem).wait()

    def start_load(p):
        def go():
            sem = load_sem.at[p % ring if isinstance(p, int) else lax.rem(p, ring)]
            pltpu.make_async_copy(la.at[p], buf.at[p, 0], sem).start()
            pltpu.make_async_copy(ra.at[p], buf.at[p, 1], sem).start()

        if not isinstance(p, int):
            pl.when(p < pairs)(go)
        elif p < pairs:
            go()

    small = [(aa, aabuf), (rka_h, rka), (ae_h, ae), (rke_h, rke)]
    rest = [
        (gpa_h, gpa), (ena_h, ena), (fka_h, fka), (nba_h, nba), (gpe_h, gpe), (ene_h, ene),
        (ine_h, ine), (fke_h, fke), (nbe_h, nbe), (ina, inbuf),
    ]
    small = [pltpu.make_async_copy(x, y, pool.at[i]) for i, (x, y) in enumerate(small)]
    rest = [pltpu.make_async_copy(x, y, pool.at[i]) for i, (x, y) in enumerate(rest)]
    for copy in small:
        copy.start()
    barrier = pltpu.get_barrier_semaphore()
    for d in order:
        pl.semaphore_signal(barrier, inc=1, device_id={"aux": lax.rem(me + d, n_aux)}, device_id_type=mesh_id)
    for d in range(1, n_pair):
        pl.semaphore_signal(barrier, inc=1, device_id={"pair": lax.rem(my_pair + d, n_pair)}, device_id_type=mesh_id)
    for q in range(pairs_e):
        pltpu.make_async_copy(le.at[q], ebuf.at[q, 0], env_sem.at[q]).start()
        pltpu.make_async_copy(re.at[q], ebuf.at[q, 1], env_sem.at[q]).start()
    for p in range(AHEAD - 2):
        start_load(p)
    for copy in small:
        copy.wait()
    for copy in rest:
        copy.start()

    def inside(rank, start, shape):
        return (start + iota2(shape, 0) < rank) & (iota2(shape, 1) < rank)

    for p in range(pairs):
        keep = inside(rka[p], me * rows, (rows, full))
        block = jnp.where(keep, aabuf[p].astype(F32), F32(0.0)).astype(BF)
        mine[p] = block
        own[me, p] = block
        around[my_pair * pairs + p] = block
    mine_e[...] = jnp.zeros(mine_e.shape, F32)
    amps_e = ae[...].astype(F32)
    for p in range(pairs_e):
        keep = inside(rke[p], me * rows_e, (rows_e, full_e))
        mine_e[p, :rows_e, :full_e] = jnp.where(keep, amps_e[:, p, :], F32(0.0))
    for p in range(pairs_e):
        around_e[my_pair * pairs_e + p] = mine_e[p]
    out_e[...] = jnp.zeros(out_e.shape, out_e.dtype)

    def remote(src, dst, send, recv, axis, peer):
        return pltpu.make_async_remote_copy(
            src_ref=src, dst_ref=dst, send_sem=send, recv_sem=recv,
            device_id={axis: peer}, device_id_type=mesh_id,
        )

    with jax.named_scope("w_barrier"):
        pl.semaphore_wait(barrier, n_aux - 1 + n_pair - 1)
    for d in order:
        remote(mine, own.at[me], send_sem.at[0], recv_sem.at[0], "aux", lax.rem(me + d, n_aux)).start()
    for d in range(1, n_pair):
        peer = lax.rem(my_pair + d, n_pair)
        remote(mine, around.at[pl.ds(my_pair * pairs, pairs)], send_sem.at[1], recv_sem.at[1], "pair", peer).start()
        remote(mine_e, around_e.at[pl.ds(my_pair * pairs_e, pairs_e)], send_sem.at[2], recv_sem.at[2], "pair", peer).start()

    def denominators(energy, gap, start, height, wide):
        line = energy + jnp.zeros((height, wide), F32)
        diag = iota2((height, wide), 1) == start + iota2((height, wide), 0)
        mine_rows = jnp.sum(jnp.where(diag, line, F32(0.0)), axis=1, keepdims=True)
        return line + mine_rows + gap

    def send_pair(p, group):
        for d in order:
            peer = lax.rem(me + d, n_aux)
            remote(out_a.at[peer, p], in_a.at[d - 1, p], pool.at[0], recv_sem.at[3 + group], "aux", peer).start()

    def ladder(p):
        with jax.named_scope("w_load"):
            landed(buf.at[p], load_sem.at[p % ring if isinstance(p, int) else lax.rem(p, ring)])
        terms[p] = dot_nt(buf[p, 0], buf[p, 1]).reshape(n_aux, rows, full)

    def prepare(p):
        left, right = half_couple(
            [inbuf[p, k] for k in range(count)],
            [around[nba[k, p]].astype(F32) for k in range(count)],
            [fka[k, p] for k in range(count)],
            me, rows, rows,
        )
        lefts[p] = left
        rights[p] = right

    def prepare_e(q):
        left, right = half_couple(
            [ine[q, k] for k in range(count)],
            [around_e[nbe[q, k]][:, :full_e] for k in range(count)],
            [fke[q, k] for k in range(count)],
            me, rows_e, pad_e,
        )
        total = terms_e[q] + dot_tn(left, right)
        for j in range(n_aux):
            out_e[j, q, :rows_e, :full_e] = total[j * rows_e : (j + 1) * rows_e, :].astype(out_e.dtype)

    def finish(p):
        base = terms[p].reshape(full, full)
        amps = own[:, p].astype(F32).reshape(full, full).astype(BF)
        half = base + dot_nt(base.astype(BF), amps)
        total = base + dot_tn(
            jnp.concatenate([amps, lefts[p]], axis=0),
            jnp.concatenate([half.astype(BF), rights[p]], axis=0),
        )
        terms[p] = total.reshape(n_aux, rows, full)
        for j in range(n_aux):
            out_a[j, p] = total[j * rows : (j + 1) * rows].astype(BF)

    def env_step(q, carry):
        landed(ebuf.at[q], env_sem.at[q])
        terms_e[q] = dot_nt(ebuf[q, 0], ebuf[q, 1])
        return carry

    half_e = pairs_e // 2
    lax.fori_loop(0, half_e, env_step, 0)
    start_load(AHEAD - 2)
    lax.fori_loop(half_e, pairs_e, env_step, 0)
    start_load(AHEAD - 1)

    def warm_step(p, carry):
        start_load(p + AHEAD)
        ladder(p)
        return carry

    lax.fori_loop(0, first, warm_step, 0)

    with jax.named_scope("w_rest"):
        for copy in rest:
            copy.wait()
    with jax.named_scope("w_pair"):
        landed(around.at[pl.ds(0, (n_pair - 1) * pairs)], recv_sem.at[1])
        landed(around_e.at[pl.ds(0, (n_pair - 1) * pairs_e)], recv_sem.at[2])

    beside = warm - first
    share, share_e = -(-pairs // beside), -(-pairs_e // beside)

    def prepare_step(i, carry):
        start_load(first + i + AHEAD)
        ladder(first + i)
        for n in range(share):
            prepare(lax.min(share * i + n, pairs - 1))
        for n in range(share_e):
            prepare_e(lax.min(share_e * i + n, pairs_e - 1))
        return carry

    lax.fori_loop(0, beside, prepare_step, 0)
    for d in order:
        peer = lax.rem(me + d, n_aux)
        remote(out_e.at[peer], in_e.at[d - 1], pool.at[1], recv_sem.at[5], "aux", peer).start()

    for p in range(pairs):
        den[p] = denominators(ena[pl.ds(p, 1), :], gpa[p], me * rows, rows, full)
    for p in range(pairs_e):
        den_e[p] = denominators(ene[pl.ds(p, 1), :], gpe[p], me * rows_e, rows_e, full_e)
    with jax.named_scope("w_own"):
        landed(own.at[pl.ds(0, n_aux - 1)], recv_sem.at[0])

    twos = min(pairs - 1 - warm, max(0, warm - 1))

    def catch_step(i, carry):
        p = warm + i
        start_load(p + AHEAD)

        @pl.when(i > 0)
        def _():
            send_pair(2 * i - 2, 0)
            send_pair(2 * i - 1, 0)

        ladder(p)
        finish(2 * i)
        finish(2 * i + 1)
        return carry

    lax.fori_loop(0, twos, catch_step, 0)
    done = 2 * twos
    sent = max(0, done - 2)
    for p in range(warm + twos, pairs):
        start_load(p + AHEAD)
        for q in range(sent, done):
            send_pair(q, int(q >= late))
        sent = done
        ladder(p)
        if done < p:
            finish(done)
            done += 1
    while done < pairs:
        for q in range(sent, done):
            send_pair(q, int(q >= late))
        sent = done
        finish(done)
        done += 1
    for p in range(sent, pairs):
        send_pair(p, int(p >= late))

    def combine(p):
        total = terms[p, me]
        for d in range(1, n_aux):
            total = total + in_a[d - 1, p].astype(F32)
        keep = inside(rka[p], me * rows, (rows, full))
        oa[p] = jnp.where(keep, mine[p].astype(F32) - total / den[p], F32(0.0))

    with jax.named_scope("w_e"):
        landed(in_e, recv_sem.at[5])
    for p in range(pairs_e):
        total = out_e[me, p].astype(F32)
        for d in range(1, n_aux):
            total = total + in_e[d - 1, p].astype(F32)
        keep = inside(rke[p], me * rows_e, (rows_e, full_e))
        oe[:, p, :] = jnp.where(
            keep, mine_e[p, :rows_e, :full_e] - total[:rows_e, :full_e] / den_e[p], F32(0.0)
        )
    with jax.named_scope("w_a0"):
        landed(in_a.at[:, pl.ds(0, late)], recv_sem.at[3])
    for p in range(late):
        combine(p)
    with jax.named_scope("w_send"):
        landed(own.at[pl.ds(0, n_aux - 1)], send_sem.at[0])
        landed(around.at[pl.ds(0, (n_pair - 1) * pairs)], send_sem.at[1])
        landed(around_e.at[pl.ds(0, (n_pair - 1) * pairs_e)], send_sem.at[2])
        landed(in_e, pool.at[1])
        landed(in_a, pool.at[0])
    with jax.named_scope("w_a1"):
        landed(in_a.at[:, pl.ds(late, pairs - late)], recv_sem.at[4])
    for p in range(late, pairs):
        combine(p)


def store(a, e, oa, oe, sem):
    copies = [pltpu.make_async_copy(a, oa, sem.at[0]), pltpu.make_async_copy(e, oe, sem.at[1])]
    for copy in copies:
        copy.start()
    for copy in copies:
        copy.wait()


def shards(n_pair, n_aux, *args):
    la, ra, aa = args[:3]
    ina = args[6]
    le, re, ae = args[9:12]
    pairs, rows, full = aa.shape
    pairs_e, rows_e, full_e = ae.shape
    pad_e = -(-rows_e // 8) * 8
    hbm = pl.BlockSpec(memory_space=pl.ANY)
    vmem = pl.BlockSpec(memory_space=pltpu.VMEM)
    dma = pltpu.SemaphoreType.DMA
    args = list(args)
    for i in (7, 8):
        args[i] = args[i].T
    args[11] = ae.transpose(1, 0, 2)

    def like(space, *which):
        return [space(args[i].shape, args[i].dtype) for i in which]

    new_a, new_e = pl.pallas_call(
        functools.partial(kernel, n_pair, n_aux),
        out_shape=(
            pltpu.VMEM(aa.shape, F32),
            pltpu.VMEM(args[11].shape, F32),
        ),
        in_specs=[hbm] * len(args),
        out_specs=(vmem, vmem),
        scratch_shapes=[
            pltpu.VMEM((pairs, 2, *la.shape[1:]), BF),
            pltpu.VMEM((pairs_e, 2, *le.shape[1:]), BF),
        ]
        + like(pltpu.VMEM, 6, 2, 11, 5, 14, 15)
        + like(pltpu.SMEM, 3, 4, 7, 8, 12, 13, 16, 17)
        + [
            pltpu.VMEM((pairs, rows, full), BF),
            pltpu.VMEM((n_aux, pairs, rows, full), BF),
            pltpu.VMEM((n_pair * pairs, rows, full), BF),
            pltpu.VMEM((pairs_e, pad_e, LANES), F32),
            pltpu.VMEM((n_pair * pairs_e, pad_e, LANES), F32),
            pltpu.VMEM((pairs, n_aux, rows, full), F32),
            pltpu.VMEM((n_aux, pairs, rows, full), BF),
            pltpu.VMEM((n_aux - 1, pairs, rows, full), BF),
            pltpu.VMEM((pairs_e, full_e, full_e), F32),
            pltpu.VMEM((n_aux, pairs_e, pad_e, LANES), EDT),
            pltpu.VMEM((n_aux - 1, pairs_e, pad_e, LANES), EDT),
            pltpu.VMEM((pairs, rows, full), F32),
            pltpu.VMEM((pairs_e, rows_e, full_e), F32),
            pltpu.VMEM((pairs, ina.shape[1] * rows, full), BF),
            pltpu.VMEM((pairs, ina.shape[1] * rows, full), BF),
            dma((AHEAD + 1,)),
            dma((pairs_e,)),
            dma((10,)),
            dma((3,)),
            dma((6,)),
        ],
        compiler_params=pltpu.CompilerParams(
            collective_id=0, has_side_effects=True, vmem_limit_bytes=60 * 1024 * 1024
        ),
        name="update",
    )(*args)
    new_a, new_e = (pltpu.with_memory_space_constraint(x, pltpu.VMEM) for x in (new_a, new_e))
    out_a, out_e = pl.pallas_call(
        store,
        out_shape=(
            jax.ShapeDtypeStruct(new_a.shape, F32),
            jax.ShapeDtypeStruct(new_e.shape, F32),
        ),
        in_specs=[vmem, vmem],
        out_specs=(hbm, hbm),
        scratch_shapes=[dma((2,))],
        name="store",
    )(new_a, new_e)
    return out_a, out_e.transpose(1, 0, 2)


def solution(mesh):
    n_pair, n_aux = mesh.shape["pair"], mesh.shape["aux"]
    level = (
        P("pair", None, "aux"),
        P("pair", None, "aux"),
        P("pair", "aux", None),
        P("pair"),
        P("pair"),
        P("pair", None),
        P("pair", None, None, None),
        P("pair", None),
        P("pair", None),
    )
    return jax.shard_map(
        functools.partial(shards, n_pair, n_aux),
        mesh=mesh,
        in_specs=level + level,
        out_specs=(P("pair", "aux", None), P("pair", "aux", None)),
        check_vma=False,
    )
```

time: 31.5 us -> 26.8 us (0.85)
  Pallas kernels: 29.5 us -> 26 us
  local copies, waits for them, and re-layouts: 1.24 us -> 0 us
    pallas_call x1, Pallas kernels: 29.5 us -> 25.4 us  [shards(): pl.pallas_call(functools.partial(kernel, n_pair, n_aux), out_shape=(pltpu...]
    unnamed x2 -> x0, local copies, waits for them, and re-layouts: 1.24 us -> none
    pallas_call x0 -> x1, Pallas kernels: none -> 0.66 us  [shards(): pl.pallas_call(store, out_shape=(jax.ShapeDtypeStruct(new_a.shape, F32),...]
where the time goes in v1:
time: 26.8 us; the launch traced here: 26.7 us
  Pallas kernels  26 us (97%)
  between operations  0.65 us (2%)
    pallas_call x1, Pallas kernels, shards(): pl.pallas_call(functools.partial(kernel, n_pair, n_aux), out_shape=(pltpu...  25.4 us
    pallas_call x1, Pallas kernels, shards(): pl.pallas_call(store, out_shape=(jax.ShapeDtypeStruct(new_a.shape, F32),...  0.66 us

profile of v1, /device:TPU:0, one launch (start us, length us, event | category | flops | bytes accessed | tf_op | source)
XLA Modules:
  0.0 26.7 jit_solution(15004305292243334591)
XLA Ops:
  0.6 25.4 %update.1 = (f32[10,16,128]{2,1,0:T(8,128)S(1)}, f32[6,4,48]{2,1,0:T(4,128)S(1)}) custom-call(bf16[10,128,7680]{2,1,0:T(8,128)(2,1)} %la.1, bf16[10,128,7680]{2,1,0:T(8,128)(2,1)} %ra.1, bf16[10,16,128]{2,1,0:T(8,128)(2,1)} %aa.1, s32[10]{0:T(128)} %rka_h.1, f32[10]{0:T(128)} %gpa_h.1, f32[10,128]{1,0:T(8,128)} %ena_h.1, bf16[10,4,128,128]{3,2,1,0:T(8,128)(2,1)} %ina.1, ...), custom_call_target="tpu_custom_call" | custom-call | tf_op jit(solution)/shard_map/update/pallas_call | solution.py:344
  26.0 0.7 %store.1 = (f32[10,16,128]{2,1,0:T(8,128)}, f32[6,4,48]{2,1,0:T(4,128)}) custom-call(f32[10,16,128]{2,1,0:T(8,128)S(1)} %get-tuple-element.6.a, f32[6,4,48]{2,1,0:T(4,128)S(1)} %get-tuple-element.7.e), custom_call_target="tpu_custom_call" | custom-call | tf_op jit(solution)/shard_map/store/pallas_call | solution.py:386

commit v2 on v1

--- a/solution.py
+++ b/solution.py
@@ -46,10 +46,6 @@
 
 def dot_tn(x, y):
     return lax.dot_general(x, y, (((0,), (0,)), ((), ())), preferred_element_type=F32)
-
-
-def far_first(n):
-    return sorted(range(1, n), key=lambda d: -min(d, n - d))
 
 
 def kernel(
@@ -73,7 +69,7 @@
     ring = load_sem.shape[0]
     me = lax.axis_index("aux")
     my_pair = lax.axis_index("pair")
-    order = far_first(n_aux)
+    order = range(1, n_aux)
     mesh_id = pl.DeviceIdType.MESH
 
     def landed(block, sem):
@@ -123,11 +119,11 @@
         mine[p] = block
         own[me, p] = block
         around[my_pair * pairs + p] = block
-    mine_e[...] = jnp.zeros(mine_e.shape, F32)
+    mine_e[...] = jnp.zeros(mine_e.shape, BF)
     amps_e = ae[...].astype(F32)
     for p in range(pairs_e):
         keep = inside(rke[p], me * rows_e, (rows_e, full_e))
-        mine_e[p, :rows_e, :full_e] = jnp.where(keep, amps_e[:, p, :], F32(0.0))
+        mine_e[p, :rows_e, :full_e] = jnp.where(keep, amps_e[:, p, :], F32(0.0)).astype(BF)
     for p in range(pairs_e):
         around_e[my_pair * pairs_e + p] = mine_e[p]
     out_e[...] = jnp.zeros(out_e.shape, out_e.dtype)
@@ -140,12 +136,12 @@
 
     with jax.named_scope("w_barrier"):
         pl.semaphore_wait(barrier, n_aux - 1 + n_pair - 1)
-    for d in order:
-        remote(mine, own.at[me], send_sem.at[0], recv_sem.at[0], "aux", lax.rem(me + d, n_aux)).start()
     for d in range(1, n_pair):
         peer = lax.rem(my_pair + d, n_pair)
         remote(mine, around.at[pl.ds(my_pair * pairs, pairs)], send_sem.at[1], recv_sem.at[1], "pair", peer).start()
         remote(mine_e, around_e.at[pl.ds(my_pair * pairs_e, pairs_e)], send_sem.at[2], recv_sem.at[2], "pair", peer).start()
+    for d in order:
+        remote(mine, own.at[me], send_sem.at[0], recv_sem.at[0], "aux", lax.rem(me + d, n_aux)).start()
 
     def denominators(energy, gap, start, height, wide):
         line = energy + jnp.zeros((height, wide), F32)
@@ -153,10 +149,13 @@
         mine_rows = jnp.sum(jnp.where(diag, line, F32(0.0)), axis=1, keepdims=True)
         return line + mine_rows + gap
 
-    def send_pair(p, group):
+    def send_pair(p, group, some=1):
         for d in order:
             peer = lax.rem(me + d, n_aux)
-            remote(out_a.at[peer, p], in_a.at[d - 1, p], pool.at[0], recv_sem.at[3 + group], "aux", peer).start()
+            remote(
+                out_a.at[peer, pl.ds(p, some)], in_a.at[d - 1, pl.ds(p, some)],
+                pool.at[0], recv_sem.at[3 + group], "aux", peer,
+            ).start()
 
     def ladder(p):
         with jax.named_scope("w_load"):
@@ -176,7 +175,7 @@
     def prepare_e(q):
         left, right = half_couple(
             [ine[q, k] for k in range(count)],
-            [around_e[nbe[q, k]][:, :full_e] for k in range(count)],
+            [around_e[nbe[q, k]].astype(F32)[:, :full_e] for k in range(count)],
             [fke[q, k] for k in range(count)],
             me, rows_e, pad_e,
         )
@@ -253,8 +252,7 @@
 
         @pl.when(i > 0)
         def _():
-            send_pair(2 * i - 2, 0)
-            send_pair(2 * i - 1, 0)
+            send_pair(2 * i - 2, 0, 2)
 
         ladder(p)
         finish(2 * i)
@@ -266,8 +264,8 @@
     sent = max(0, done - 2)
     for p in range(warm + twos, pairs):
         start_load(p + AHEAD)
-        for q in range(sent, done):
-            send_pair(q, int(q >= late))
+        if sent < done:
+            send_pair(sent, int(sent >= late), done - sent)
         sent = done
         ladder(p)
         if done < p:
@@ -297,7 +295,7 @@
             total = total + in_e[d - 1, p].astype(F32)
         keep = inside(rke[p], me * rows_e, (rows_e, full_e))
         oe[:, p, :] = jnp.where(
-            keep, mine_e[p, :rows_e, :full_e] - total[:rows_e, :full_e] / den_e[p], F32(0.0)
+            keep, mine_e[p].astype(F32)[:rows_e, :full_e] - total[:rows_e, :full_e] / den_e[p], F32(0.0)
         )
     with jax.named_scope("w_a0"):
         landed(in_a.at[:, pl.ds(0, late)], recv_sem.at[3])
@@ -359,8 +357,8 @@
             pltpu.VMEM((pairs, rows, full), BF),
             pltpu.VMEM((n_aux, pairs, rows, full), BF),
             pltpu.VMEM((n_pair * pairs, rows, full), BF),
-            pltpu.VMEM((pairs_e, pad_e, LANES), F32),
-            pltpu.VMEM((n_pair * pairs_e, pad_e, LANES), F32),
+            pltpu.VMEM((pairs_e, pad_e, LANES), BF),
+            pltpu.VMEM((n_pair * pairs_e, pad_e, LANES), BF),
             pltpu.VMEM((pairs, n_aux, rows, full), F32),
             pltpu.VMEM((n_aux, pairs, rows, full), BF),
             pltpu.VMEM((n_aux - 1, pairs, rows, full), BF),

time: 26.8 us -> 26.8 us (level)
  no operation moved by 1% of the time
where the time goes in v2:
time: 26.8 us; the launch traced here: 26.7 us
  Pallas kernels  26 us (97%)
  between operations  0.65 us (2%)
    pallas_call x1, Pallas kernels, shards(): pl.pallas_call(functools.partial(kernel, n_pair, n_aux), out_shape=(pltpu...  25.4 us
    pallas_call x1, Pallas kernels, shards(): pl.pallas_call(store, out_shape=(jax.ShapeDtypeStruct(new_a.shape, F32),...  0.66 us

profile of v2, /device:TPU:0, one launch (start us, length us, event | category | flops | bytes accessed | tf_op | source)
XLA Modules:
  0.0 26.7 jit_solution(4387655143486014778)
XLA Ops:
  0.6 25.4 %update.1 = (f32[10,16,128]{2,1,0:T(8,128)S(1)}, f32[6,4,48]{2,1,0:T(4,128)S(1)}) custom-call(bf16[10,128,7680]{2,1,0:T(8,128)(2,1)} %la.1, bf16[10,128,7680]{2,1,0:T(8,128)(2,1)} %ra.1, bf16[10,16,128]{2,1,0:T(8,128)(2,1)} %aa.1, s32[10]{0:T(128)} %rka_h.1, f32[10]{0:T(128)} %gpa_h.1, f32[10,128]{1,0:T(8,128)} %ena_h.1, bf16[10,4,128,128]{3,2,1,0:T(8,128)(2,1)} %ina.1, ...), custom_call_target="tpu_custom_call" | custom-call | tf_op jit(solution)/shard_map/update/pallas_call | solution.py:342
  26.0 0.7 %store.1 = (f32[10,16,128]{2,1,0:T(8,128)}, f32[6,4,48]{2,1,0:T(4,128)}) custom-call(f32[10,16,128]{2,1,0:T(8,128)S(1)} %get-tuple-element.6.a, f32[6,4,48]{2,1,0:T(4,128)S(1)} %get-tuple-element.7.e), custom_call_target="tpu_custom_call" | custom-call | tf_op jit(solution)/shard_map/store/pallas_call | solution.py:384
